TPU v7x, 32 devices: a whole 2x2x4 slice. The times are simulated.
32 devices in a mesh: row: 16 (over z, x, core), ch: 2 (over y).
Axes of the slice: x: 2, y: 2, z: 4, core: 2. Of those that a mesh axis runs over, the one named last changes fastest.
Arguments:
- pair_rep: float32 [256, 256, 128], P('row', 'ch'), may hold values from -6 to 6
- residue_mask: int32 [256], replicated, may hold values 0 or 1
- pair_gain: float32 [2, 128], replicated, may hold values from 0.5 to 1.5
- pair_shift: float32 [2, 128], replicated, may hold values from -3 to 3
- panel_weight: bfloat16 [2, 128, 512], replicated, may hold values from -0.5 to 0.5
- panel_bias: float32 [2, 512], replicated, may hold values from -3 to 3
- gate_weight: bfloat16 [2, 128, 128], replicated, may hold values from -0.5 to 0.5
- gate_bias: float32 [2, 128], replicated, may hold values from -3 to 3
- hidden_gain: float32 [2, 128], replicated, may hold values from 0.5 to 1.5
- hidden_shift: float32 [2, 128], replicated, may hold values from -3 to 3
- output_weight: bfloat16 [2, 128, 128], replicated, may hold values from -0.5 to 0.5
- output_bias: float32 [2, 128], replicated, may hold values from -3 to 3
Outputs:
- updated_pair: float32 [256, 256, 128], P('row', 'ch')
All inputs are finite; a program needn't handle non-finite values.
Results may differ from a plain program's by a relative error of at most 0.0039.
Values may be sent and summed in bfloat16 or wider, within the bound.
A program may use at most 64 MiB of HBM per device.

v0:
```python
import jax
import jax.numpy as jnp
from jax import lax
from jax.sharding import PartitionSpec as P

PAIR_EPSILON = 1e-05
HIDDEN_EPSILON = 1.0


def layer_norm(values, gain_value, shift_value, along, epsilon):
    center = jnp.mean(values, axis=along, keepdims=True)
    offset = values - center
    spread = jnp.mean(offset * offset, axis=along, keepdims=True)
    return offset * lax.rsqrt(spread + epsilon) * gain_value + shift_value


def project(
    current,
    cell_mask,
    section_index,
    pair_gain,
    pair_shift,
    panel_weight,
    panel_bias,
    gate_weight,
    gate_bias,
):
    normed = layer_norm(
        current, pair_gain[section_index], pair_shift[section_index], 2, PAIR_EPSILON
    ).astype(jnp.bfloat16)
    hidden_width = panel_weight.shape[2] // 4
    features = jnp.einsum(
        "rjc,cf->frj", normed, panel_weight[section_index], preferred_element_type=jnp.float32
    )
    features = features + panel_bias[section_index][:, None, None]
    left_panel = (
        cell_mask
        * jax.nn.sigmoid(features[:hidden_width])
        * features[hidden_width : 2 * hidden_width]
    ).astype(jnp.bfloat16)
    right_panel = (
        cell_mask
        * jax.nn.sigmoid(features[2 * hidden_width : 3 * hidden_width])
        * features[3 * hidden_width :]
    ).astype(jnp.bfloat16)
    gate_value = jax.nn.sigmoid(
        jnp.einsum(
            "rjc,cd->rjd", normed, gate_weight[section_index], preferred_element_type=jnp.float32
        )
        + gate_bias[section_index]
    )
    return (left_panel, right_panel, gate_value)


def local(
    pair_rep,
    residue_mask,
    pair_gain,
    pair_shift,
    panel_weight,
    panel_bias,
    gate_weight,
    gate_bias,
    hidden_gain,
    hidden_shift,
    output_weight,
    output_bias,
):
    row_count = pair_rep.shape[0]
    col_count = pair_rep.shape[1]
    hidden_width = panel_weight.shape[2] // 4
    row_total = lax.axis_size("row")
    col_total = lax.axis_size("ch")
    group = hidden_width // col_total
    if group >= row_total:
        per_slot = group // row_total
        quarters = 1
    else:
        per_slot = 1
        quarters = row_total // group
    slots = row_total // quarters
    sub_rows = row_count // quarters
    blocks = col_count // row_count
    row_index = lax.axis_index("row")
    col_index = lax.axis_index("ch")
    residue_float = residue_mask.astype(jnp.float32)
    row_mask = lax.dynamic_slice_in_dim(residue_float, row_index * row_count, row_count)
    col_mask = lax.dynamic_slice_in_dim(residue_float, col_index * col_count, col_count)
    cell_mask = row_mask[:, None] * col_mask[None, :]
    current = pair_rep
    for section_index in range(2):
        left_panel, right_panel, gate_value = project(
            current,
            cell_mask,
            section_index,
            pair_gain,
            pair_shift,
            panel_weight,
            panel_bias,
            gate_weight,
            gate_bias,
        )
        if section_index == 0:
            send_left = left_panel.reshape(
                col_total, slots, per_slot, quarters, sub_rows, col_count
            )
            send_left = jnp.transpose(send_left, (0, 1, 3, 2, 4, 5)).reshape(
                col_total, row_total, per_slot, sub_rows, col_count
            )
        else:
            send_left = left_panel.reshape(
                col_total, slots, per_slot, row_count, blocks, quarters, sub_rows
            )
            send_left = jnp.transpose(send_left, (0, 1, 5, 2, 3, 4, 6)).reshape(
                col_total, row_total, per_slot, row_count, blocks * sub_rows
            )
        send_right = right_panel.reshape(col_total, slots, 1, per_slot, row_count, col_count)
        send_right = jnp.broadcast_to(
            send_right, (col_total, slots, quarters, per_slot, row_count, col_count)
        ).reshape(col_total, row_total, per_slot, row_count, col_count)
        got_left, got_right = (
            lax.all_to_all(
                lax.all_to_all(send_left, "ch", split_axis=0, concat_axis=4, tiled=True),
                "row",
                split_axis=1,
                concat_axis=3,
                tiled=True,
            ),
            lax.all_to_all(
                lax.all_to_all(send_right, "ch", split_axis=0, concat_axis=4, tiled=True),
                "row",
                split_axis=1,
                concat_axis=3,
                tiled=True,
            ),
        )
        got_left = got_left[0, 0]
        got_right = got_right[0, 0]
        if section_index == 0:
            products = jnp.einsum(
                "hik,hjk->hij", got_left, got_right, preferred_element_type=jnp.float32
            )
        else:
            products = jnp.einsum(
                "hki,hkj->hij", got_left, got_right, preferred_element_type=jnp.float32
            )
        returned = products.reshape(per_slot, row_total, sub_rows, col_total, col_count)
        gathered = lax.all_to_all(
            lax.all_to_all(returned, "row", split_axis=1, concat_axis=0, tiled=True),
            "ch",
            split_axis=3,
            concat_axis=0,
            tiled=True,
        )
        gathered = gathered.reshape(col_total, slots, quarters, per_slot, sub_rows, col_count)
        gathered = jnp.transpose(gathered, (0, 1, 3, 2, 4, 5)).reshape(
            hidden_width, row_count, col_count
        )
        normed = layer_norm(
            gathered,
            hidden_gain[section_index][:, None, None],
            hidden_shift[section_index][:, None, None],
            0,
            HIDDEN_EPSILON,
        ).astype(jnp.bfloat16)
        projected = jnp.einsum(
            "hrj,hc->rjc", normed, output_weight[section_index], preferred_element_type=jnp.float32
        )
        current = current + gate_value * (projected + output_bias[section_index])
    return current


def solution(mesh):
    return jax.shard_map(
        local,
        mesh=mesh,
        in_specs=(P("row", "ch", None), P(), P(), P(), P(), P(), P(), P(), P(), P(), P(), P()),
        out_specs=P("row", "ch", None),
        check_vma=False,
    )
```

profile of v0, /device:TPU:0, one launch (start us, length us, event | category | flops | bytes accessed | tf_op | source)
XLA Modules:
  0.0 238.2 jit_solution(15132575258035576822)
XLA Ops:
  0.8 1.6 reduce_sum.72
  2.4 1.9 multiply_reduce_fusion.3
  6.7 2.1 add_bitcast_fusion.1
  9.4 1.2 copy.82
  10.6 4.3 %all-to-all-start = ((bf16[2,16,4,16,128]{4,3,2,1,0:T(8,128)(2,1)}), bf16[2,16,4,16,128]{4,3,2,1,0:T(8,128)(2,1)S(1)}, u32[]{:S(2)}, u32[]{:S(2)}) async-start(bf16[2,16,4,16,128]{4,3,2,1,0:T(8,128)(2,1)} %bitcast.9), calls=%async_computation | async-start | bytes 1048576 | tf_op jit(solution)/shard_map/all_to_all | solution.py:123
  14.9 1.2 copy.86
  16.0 7.5 %all-to-all-done = bf16[2,16,4,16,128]{4,3,2,1,0:T(8,128)(2,1)S(1)} async-done(((bf16[2,16,4,16,128]{4,3,2,1,0:T(8,128)(2,1)}), bf16[2,16,4,16,128]{4,3,2,1,0:T(8,128)(2,1)S(1)}, u32[]{:S(2)}, u32[]{:S(2)}) %all-to-all-start) | async-done | bytes 524320 | tf_op jit(solution)/shard_map/all_to_all | solution.py:123
  23.6 3.5 %all-to-all-start.2 = ((bf16[2,16,4,16,128]{4,3,2,1,0:T(8,128)(2,1)}), bf16[2,16,4,16,128]{4,3,2,1,0:T(8,128)(2,1)S(1)}, u32[]{:S(2)}, u32[]{:S(2)}) async-start(bf16[2,16,4,16,128]{4,3,2,1,0:T(8,128)(2,1)} %bitcast.16), calls=%async_computation.2 | async-start | bytes 1048576 | tf_op jit(solution)/shard_map/all_to_all | solution.py:130
  28.0 6.8 %all-to-all-done.2 = bf16[2,16,4,16,128]{4,3,2,1,0:T(8,128)(2,1)S(1)} async-done(((bf16[2,16,4,16,128]{4,3,2,1,0:T(8,128)(2,1)}), bf16[2,16,4,16,128]{4,3,2,1,0:T(8,128)(2,1)S(1)}, u32[]{:S(2)}, u32[]{:S(2)}) %all-to-all-start.2) | async-done | bytes 524320 | tf_op jit(solution)/shard_map/all_to_all | solution.py:130
  34.7 5.9 %all-to-all-start.1 = ((bf16[1,16,4,16,256]{4,3,2,0,1:T(8,128)(2,1)}), bf16[1,16,4,16,256]{4,3,2,0,1:T(8,128)(2,1)S(1)}, u32[]{:S(2)}, u32[]{:S(2)}) async-start(bf16[1,16,4,16,256]{4,3,2,0,1:T(8,128)(2,1)} %bitcast_bitcast_fusion.3), calls=%async_computation.1 | async-start | bytes 1048576 | tf_op jit(solution)/shard_map/all_to_all | solution.py:122
  41.5 13.4 %all-to-all-done.1 = bf16[1,16,4,16,256]{4,3,2,0,1:T(8,128)(2,1)S(1)} async-done(((bf16[1,16,4,16,256]{4,3,2,0,1:T(8,128)(2,1)}), bf16[1,16,4,16,256]{4,3,2,0,1:T(8,128)(2,1)S(1)}, u32[]{:S(2)}, u32[]{:S(2)}) %all-to-all-start.1) | async-done | bytes 524320 | tf_op jit(solution)/shard_map/all_to_all | solution.py:122
  54.9 4.2 %all-to-all-start.3 = ((bf16[1,16,4,16,256]{4,3,2,0,1:T(8,128)(2,1)}), bf16[1,16,4,16,256]{4,3,2,0,1:T(8,128)(2,1)S(1)}, u32[]{:S(2)}, u32[]{:S(2)}) async-start(bf16[1,16,4,16,256]{4,3,2,0,1:T(8,128)(2,1)} %bitcast_bitcast_fusion.2), calls=%async_computation.3 | async-start | bytes 1048576 | tf_op jit(solution)/shard_map/all_to_all | solution.py:129
  59.1 14.2 %all-to-all-done.3 = bf16[1,16,4,16,256]{4,3,2,0,1:T(8,128)(2,1)S(1)} async-done(((bf16[1,16,4,16,256]{4,3,2,0,1:T(8,128)(2,1)}), bf16[1,16,4,16,256]{4,3,2,0,1:T(8,128)(2,1)S(1)}, u32[]{:S(2)}, u32[]{:S(2)}) %all-to-all-start.3) | async-done | bytes 524320 | tf_op jit(solution)/shard_map/all_to_all | solution.py:129
  74.4 28.8 %all_to_all.198 = f32[4,16,16,2,128]{4,2,3,0,1:T(8,128)S(1)} all-to-all(f32[4,16,16,2,128]{4,2,3,0,1:T(8,128)S(1)} %copy.90), channel_id=1, replica_groups=mesh['row'=16,'ch'=2] {'row'}, dimensions={1} | all-to-all | bytes 2097152 | tf_op jit(solution)/shard_map/all_to_all | solution.py:149
  103.2 1.1 copy.91
  104.3 3.6 %all-to-all-start.5 = ((f32[64,1,16,2,128]{4,2,1,0,3:T(8,128)}), f32[64,1,16,2,128]{4,2,1,0,3:T(8,128)S(1)}, u32[]{:S(2)}, u32[]{:S(2)}) async-start(f32[64,1,16,2,128]{4,2,1,0,3:T(8,128)} %copy.91), calls=%async_computation.5 | async-start | bytes 2097152 | tf_op jit(solution)/shard_map/all_to_all | solution.py:148
  108.4 2.0 fusion.11
  110.4 12.4 %all-to-all-done.5 = f32[64,1,16,2,128]{4,2,1,0,3:T(8,128)S(1)} async-done(((f32[64,1,16,2,128]{4,2,1,0,3:T(8,128)}), f32[64,1,16,2,128]{4,2,1,0,3:T(8,128)S(1)}, u32[]{:S(2)}, u32[]{:S(2)}) %all-to-all-start.5) | async-done | bytes 1048608 | tf_op jit(solution)/shard_map/all_to_all | solution.py:148
  126.0 1.2 copy.102
  127.2 3.5 %all-to-all-start.8 = ((bf16[2,16,4,16,128]{4,3,2,1,0:T(8,128)(2,1)}), bf16[2,16,4,16,128]{4,3,2,1,0:T(8,128)(2,1)S(1)}, u32[]{:S(2)}, u32[]{:S(2)}) async-start(bf16[2,16,4,16,128]{4,3,2,1,0:T(8,128)(2,1)} %bitcast.49), calls=%async_computation.8 | async-start | bytes 1048576 | tf_op jit(solution)/shard_map/all_to_all | solution.py:130
  130.7 1.2 copy.98
  131.9 7.3 %all-to-all-done.8 = bf16[2,16,4,16,128]{4,3,2,1,0:T(8,128)(2,1)S(1)} async-done(((bf16[2,16,4,16,128]{4,3,2,1,0:T(8,128)(2,1)}), bf16[2,16,4,16,128]{4,3,2,1,0:T(8,128)(2,1)S(1)}, u32[]{:S(2)}, u32[]{:S(2)}) %all-to-all-start.8) | async-done | bytes 524320 | tf_op jit(solution)/shard_map/all_to_all | solution.py:130
  139.2 3.5 %all-to-all-start.6 = ((bf16[2,16,4,16,128]{4,3,2,1,0:T(8,128)(2,1)}), bf16[2,16,4,16,128]{4,3,2,1,0:T(8,128)(2,1)S(1)}, u32[]{:S(2)}, u32[]{:S(2)}) async-start(bf16[2,16,4,16,128]{4,3,2,1,0:T(8,128)(2,1)} %bitcast.42), calls=%async_computation.6 | async-start | bytes 1048576 | tf_op jit(solution)/shard_map/all_to_all | solution.py:123
  143.6 6.8 %all-to-all-done.6 = bf16[2,16,4,16,128]{4,3,2,1,0:T(8,128)(2,1)S(1)} async-done(((bf16[2,16,4,16,128]{4,3,2,1,0:T(8,128)(2,1)}), bf16[2,16,4,16,128]{4,3,2,1,0:T(8,128)(2,1)S(1)}, u32[]{:S(2)}, u32[]{:S(2)}) %all-to-all-start.6) | async-done | bytes 524320 | tf_op jit(solution)/shard_map/all_to_all | solution.py:123
  150.4 3.6 %all-to-all-start.9 = ((bf16[1,16,4,16,256]{4,3,2,0,1:T(8,128)(2,1)}), bf16[1,16,4,16,256]{4,3,2,0,1:T(8,128)(2,1)S(1)}, u32[]{:S(2)}, u32[]{:S(2)}) async-start(bf16[1,16,4,16,256]{4,3,2,0,1:T(8,128)(2,1)} %bitcast_bitcast_fusion), calls=%async_computation.9 | async-start | bytes 1048576 | tf_op jit(solution)/shard_map/all_to_all | solution.py:129
  154.8 13.4 %all-to-all-done.9 = bf16[1,16,4,16,256]{4,3,2,0,1:T(8,128)(2,1)S(1)} async-done(((bf16[1,16,4,16,256]{4,3,2,0,1:T(8,128)(2,1)}), bf16[1,16,4,16,256]{4,3,2,0,1:T(8,128)(2,1)S(1)}, u32[]{:S(2)}, u32[]{:S(2)}) %all-to-all-start.9) | async-done | bytes 524320 | tf_op jit(solution)/shard_map/all_to_all | solution.py:129
  168.2 4.1 %all-to-all-start.7 = ((bf16[1,16,4,16,256]{4,3,2,0,1:T(8,128)(2,1)}), bf16[1,16,4,16,256]{4,3,2,0,1:T(8,128)(2,1)S(1)}, u32[]{:S(2)}, u32[]{:S(2)}) async-start(bf16[1,16,4,16,256]{4,3,2,0,1:T(8,128)(2,1)} %bitcast_bitcast_fusion.1), calls=%async_computation.7 | async-start | bytes 1048576 | tf_op jit(solution)/shard_map/all_to_all | solution.py:122
  172.3 14.2 %all-to-all-done.7 = bf16[1,16,4,16,256]{4,3,2,0,1:T(8,128)(2,1)S(1)} async-done(((bf16[1,16,4,16,256]{4,3,2,0,1:T(8,128)(2,1)}), bf16[1,16,4,16,256]{4,3,2,0,1:T(8,128)(2,1)S(1)}, u32[]{:S(2)}, u32[]{:S(2)}) %all-to-all-start.7) | async-done | bytes 524320 | tf_op jit(solution)/shard_map/all_to_all | solution.py:122
  187.6 28.6 %all_to_all.199 = f32[4,16,16,2,128]{4,2,3,0,1:T(8,128)S(1)} all-to-all(f32[4,16,16,2,128]{4,2,3,0,1:T(8,128)S(1)} %copy.107), channel_id=1, replica_groups=mesh['row'=16,'ch'=2] {'row'}, dimensions={1} | all-to-all | bytes 2097152 | tf_op jit(solution)/shard_map/all_to_all | solution.py:149
  217.3 3.6 %all-to-all-start.11 = ((f32[64,1,16,2,128]{4,2,1,0,3:T(8,128)}), f32[64,1,16,2,128]{4,2,1,0,3:T(8,128)S(1)}, u32[]{:S(2)}, u32[]{:S(2)}) async-start(f32[64,1,16,2,128]{4,2,1,0,3:T(8,128)} %copy.108), calls=%async_computation.11 | async-start | bytes 2097152 | tf_op jit(solution)/shard_map/all_to_all | solution.py:148
  221.6 14.3 %all-to-all-done.11 = f32[64,1,16,2,128]{4,2,1,0,3:T(8,128)S(1)} async-done(((f32[64,1,16,2,128]{4,2,1,0,3:T(8,128)}), f32[64,1,16,2,128]{4,2,1,0,3:T(8,128)S(1)}, u32[]{:S(2)}, u32[]{:S(2)}) %all-to-all-start.11) | async-done | bytes 1048608 | tf_op jit(solution)/shard_map/all_to_all | solution.py:148
  236.9 1.3 copy.111
  (68 shorter events, 15.8 us)
Async XLA Ops:
  10.6 13.0 %all-to-all-start = ((bf16[2,16,4,16,128]{4,3,2,1,0:T(8,128)(2,1)}), bf16[2,16,4,16,128]{4,3,2,1,0:T(8,128)(2,1)S(1)}, u32[]{:S(2)}, u32[]{:S(2)}) async-start(bf16[2,16,4,16,128]{4,3,2,1,0:T(8,128)(2,1)} %bitcast.9), calls=%async_computation | async-start | bytes 1048576 | tf_op jit(solution)/shard_map/all_to_all | solution.py:123
  23.6 11.2 %all-to-all-start.2 = ((bf16[2,16,4,16,128]{4,3,2,1,0:T(8,128)(2,1)}), bf16[2,16,4,16,128]{4,3,2,1,0:T(8,128)(2,1)S(1)}, u32[]{:S(2)}, u32[]{:S(2)}) async-start(bf16[2,16,4,16,128]{4,3,2,1,0:T(8,128)(2,1)} %bitcast.16), calls=%async_computation.2 | async-start | bytes 1048576 | tf_op jit(solution)/shard_map/all_to_all | solution.py:130
  34.7 20.1 %all-to-all-start.1 = ((bf16[1,16,4,16,256]{4,3,2,0,1:T(8,128)(2,1)}), bf16[1,16,4,16,256]{4,3,2,0,1:T(8,128)(2,1)S(1)}, u32[]{:S(2)}, u32[]{:S(2)}) async-start(bf16[1,16,4,16,256]{4,3,2,0,1:T(8,128)(2,1)} %bitcast_bitcast_fusion.3), calls=%async_computation.1 | async-start | bytes 1048576 | tf_op jit(solution)/shard_map/all_to_all | solution.py:122
  54.9 18.4 %all-to-all-start.3 = ((bf16[1,16,4,16,256]{4,3,2,0,1:T(8,128)(2,1)}), bf16[1,16,4,16,256]{4,3,2,0,1:T(8,128)(2,1)S(1)}, u32[]{:S(2)}, u32[]{:S(2)}) async-start(bf16[1,16,4,16,256]{4,3,2,0,1:T(8,128)(2,1)} %bitcast_bitcast_fusion.2), calls=%async_computation.3 | async-start | bytes 1048576 | tf_op jit(solution)/shard_map/all_to_all | solution.py:129
  74.3 33.6 %copy-start.5 = (f32[2,128]{1,0:T(2,128)S(1)}, f32[2,128]{1,0:T(2,128)}, u32[]{:S(2)}) copy-start(f32[2,128]{1,0:T(2,128)} %param.21) | copy-start | bytes 3076
  74.3 33.6 %copy-start.6 = (f32[2,128]{1,0:T(2,128)S(1)}, f32[2,128]{1,0:T(2,128)}, u32[]{:S(2)}) copy-start(f32[2,128]{1,0:T(2,128)} %param.20) | copy-start | bytes 3076
  74.3 33.6 %copy-start = (f32[16,128,128]{2,1,0:T(8,128)S(1)}, f32[16,128,128]{2,1,0:T(8,128)}, u32[]{:S(2)}) copy-start(f32[16,128,128]{2,1,0:T(8,128)} %param.12) | copy-start | bytes 3145732
  74.4 34.0 %copy-start.4 = (f32[2,128]{1,0:T(2,128)S(1)}, f32[2,128]{1,0:T(2,128)}, u32[]{:S(2)}) copy-start(f32[2,128]{1,0:T(2,128)} %param.23) | copy-start | bytes 3076
  74.4 34.0 %copy-start.7 = (bf16[2,128,128]{2,1,0:T(8,128)(2,1)S(1)}, bf16[2,128,128]{2,1,0:T(8,128)(2,1)}, u32[]{:S(2)}) copy-start(bf16[2,128,128]{2,1,0:T(8,128)(2,1)} %param.18) | copy-start | bytes 196612
  104.3 18.6 %all-to-all-start.5 = ((f32[64,1,16,2,128]{4,2,1,0,3:T(8,128)}), f32[64,1,16,2,128]{4,2,1,0,3:T(8,128)S(1)}, u32[]{:S(2)}, u32[]{:S(2)}) async-start(f32[64,1,16,2,128]{4,2,1,0,3:T(8,128)} %copy.91), calls=%async_computation.5 | async-start | bytes 2097152 | tf_op jit(solution)/shard_map/all_to_all | solution.py:148
  108.4 15.1 %copy-start.3 = (bf16[2,128,128]{2,1,0:T(8,128)(2,1)S(1)}, bf16[2,128,128]{2,1,0:T(8,128)(2,1)}, u32[]{:S(2)}) copy-start(bf16[2,128,128]{2,1,0:T(8,128)(2,1)} %param.22) | copy-start | bytes 196612
  110.4 14.1 %copy-start.2 = (bf16[2,128,512]{2,1,0:T(8,128)(2,1)S(1)}, bf16[2,128,512]{2,1,0:T(8,128)(2,1)}, u32[]{:S(2)}) copy-start(bf16[2,128,512]{2,1,0:T(8,128)(2,1)} %param.16) | copy-start | bytes 786436
  122.8 1.2 copy-start.1
  127.2 12.0 %all-to-all-start.8 = ((bf16[2,16,4,16,128]{4,3,2,1,0:T(8,128)(2,1)}), bf16[2,16,4,16,128]{4,3,2,1,0:T(8,128)(2,1)S(1)}, u32[]{:S(2)}, u32[]{:S(2)}) async-start(bf16[2,16,4,16,128]{4,3,2,1,0:T(8,128)(2,1)} %bitcast.49), calls=%async_computation.8 | async-start | bytes 1048576 | tf_op jit(solution)/shard_map/all_to_all | solution.py:130
  139.2 11.2 %all-to-all-start.6 = ((bf16[2,16,4,16,128]{4,3,2,1,0:T(8,128)(2,1)}), bf16[2,16,4,16,128]{4,3,2,1,0:T(8,128)(2,1)S(1)}, u32[]{:S(2)}, u32[]{:S(2)}) async-start(bf16[2,16,4,16,128]{4,3,2,1,0:T(8,128)(2,1)} %bitcast.42), calls=%async_computation.6 | async-start | bytes 1048576 | tf_op jit(solution)/shard_map/all_to_all | solution.py:123
  150.4 17.8 %all-to-all-start.9 = ((bf16[1,16,4,16,256]{4,3,2,0,1:T(8,128)(2,1)}), bf16[1,16,4,16,256]{4,3,2,0,1:T(8,128)(2,1)S(1)}, u32[]{:S(2)}, u32[]{:S(2)}) async-start(bf16[1,16,4,16,256]{4,3,2,0,1:T(8,128)(2,1)} %bitcast_bitcast_fusion), calls=%async_computation.9 | async-start | bytes 1048576 | tf_op jit(solution)/shard_map/all_to_all | solution.py:129
  168.2 18.4 %all-to-all-start.7 = ((bf16[1,16,4,16,256]{4,3,2,0,1:T(8,128)(2,1)}), bf16[1,16,4,16,256]{4,3,2,0,1:T(8,128)(2,1)S(1)}, u32[]{:S(2)}, u32[]{:S(2)}) async-start(bf16[1,16,4,16,256]{4,3,2,0,1:T(8,128)(2,1)} %bitcast_bitcast_fusion.1), calls=%async_computation.7 | async-start | bytes 1048576 | tf_op jit(solution)/shard_map/all_to_all | solution.py:122
  187.5 33.6 %copy-start.8 = (bf16[2,128,128]{2,1,0:T(8,128)(2,1)S(1)}, bf16[2,128,128]{2,1,0:T(8,128)(2,1)}, u32[]{:S(2)}) copy-start(bf16[2,128,128]{2,1,0:T(8,128)(2,1)} %param.18) | copy-start | bytes 196612
  217.3 18.6 %all-to-all-start.11 = ((f32[64,1,16,2,128]{4,2,1,0,3:T(8,128)}), f32[64,1,16,2,128]{4,2,1,0,3:T(8,128)S(1)}, u32[]{:S(2)}, u32[]{:S(2)}) async-start(f32[64,1,16,2,128]{4,2,1,0,3:T(8,128)} %copy.108), calls=%async_computation.11 | async-start | bytes 2097152 | tf_op jit(solution)/shard_map/all_to_all | solution.py:148
where the time goes:
time: 240 us; the launch traced here: 238 us
  waiting for transfers between devices  110 us (46%)
  blocking collectives  57.4 us (24%)
  starting transfers between devices  39.6 us (16%)
  local copies, waits for them, and re-layouts  16.7 us (7%)
  matrix products  6.89 us (3%)
  other arithmetic  6.83 us (3%)
    all_to_all x2, blocking collectives, local(): lax.all_to_all(returned, 'row', split_axis=1, concat_axis=0, tiled=True)  57.4 us
    all_to_all x2, waiting for transfers between devices, local(): lax.all_to_all(lax.all_to_all(send_left, 'ch', split_axis=0, concat_axis=...  27.6 us
    all_to_all x2, waiting for transfers between devices, local(): lax.all_to_all(lax.all_to_all(send_right, 'ch', split_axis=0, concat_axis...  27.6 us
    all_to_all x2, waiting for transfers between devices, local(): lax.all_to_all(lax.all_to_all(returned, 'row', split_axis=1, concat_axis=...  26.7 us
    all_to_all x2, waiting for transfers between devices, local(): lax.all_to_all(send_left, 'ch', split_axis=0, concat_axis=4, tiled=True)  14.4 us
    all_to_all x2, waiting for transfers between devices, local(): lax.all_to_all(send_right, 'ch', split_axis=0, concat_axis=4, tiled=True)  14.1 us
    all_to_all x2, starting transfers between devices, local(): lax.all_to_all(lax.all_to_all(send_left, 'ch', split_axis=0, concat_axis=...  9.96 us
    all_to_all x2, starting transfers between devices, local(): lax.all_to_all(send_left, 'ch', split_axis=0, concat_axis=4, tiled=True)  7.75 us
  transfers between devices with their start and end apart: 10, of which 10 were waited for; matrix products, arithmetic and copies ran while one was open for 4% of the time, Pallas kernels for 0%

commit v1 on v0

--- a/solution.py
+++ b/solution.py
@@ -5,6 +5,28 @@
 
 PAIR_EPSILON = 1e-05
 HIDDEN_EPSILON = 1.0
+
+
+def split_up(shard, dim, size):
+    before, after = (shard.shape[:dim], shard.shape[dim + 1 :])
+    return jnp.moveaxis(shard.reshape(*before, size, -1, *after), dim, 0)
+
+
+def laid_out(parts, dim):
+    lengths = list(parts.shape[1:])
+    lengths[dim] *= parts.shape[0]
+    return jnp.moveaxis(parts, 0, dim).reshape(lengths)
+
+
+def exchange_in_pairs(x, axis, split_dim, concat_dim):
+    size, mine = (lax.axis_size(axis), lax.axis_index(axis))
+    blocks = split_up(x, split_dim, size)
+    done = [blocks[mine]]
+    for step in range(1, size):
+        sent = blocks[mine ^ step]
+        done.append(lax.ppermute(sent, axis, [(i, i ^ step) for i in range(size)]))
+    blocks = jnp.stack(done)[mine ^ jnp.arange(size)]
+    return laid_out(blocks, concat_dim)
 
 
 def layer_norm(values, gain_value, shift_value, along, epsilon):
@@ -146,11 +168,7 @@
             )
         returned = products.reshape(per_slot, row_total, sub_rows, col_total, col_count)
         gathered = lax.all_to_all(
-            lax.all_to_all(returned, "row", split_axis=1, concat_axis=0, tiled=True),
-            "ch",
-            split_axis=3,
-            concat_axis=0,
-            tiled=True,
+            exchange_in_pairs(returned, "row", 1, 0), "ch", split_axis=3, concat_axis=0, tiled=True
         )
         gathered = gathered.reshape(col_total, slots, quarters, per_slot, sub_rows, col_count)
         gathered = jnp.transpose(gathered, (0, 1, 3, 2, 4, 5)).reshape(

time: 240 us -> 247 us (1.029)
  blocking collectives: 57.4 us -> 0 us
  starting transfers between devices: 39.6 us -> 83.3 us
  waiting for transfers between devices: 110 us -> 125 us
  local copies, waits for them, and re-layouts: 16.7 us -> 20.2 us
    all_to_all x2 -> x0, blocking collectives: 57.4 us -> none  [local(): lax.all_to_all(returned, 'row', split_axis=1, concat_axis=0, tiled=True)]
    ppermute x0 -> x30, starting transfers between devices: none -> 41.8 us  [exchange_in_pairs(): done.append(lax.ppermute(sent, axis, [(i, i ^ step) for i in range(size)]))]
    ppermute x0 -> x30, waiting for transfers between devices: none -> 19.9 us  [exchange_in_pairs(): done.append(lax.ppermute(sent, axis, [(i, i ^ step) for i in range(size)]))]
  transfers between devices with their start and end apart: 10 -> 40, of which waited for: 10 -> 18; matrix products, arithmetic and copies ran while one was open for 4% -> 5% of each run, Pallas kernels for 0% -> 0%
where the time goes in v1:
time: 247 us; the launch traced here: 245 us
  waiting for transfers between devices  125 us (51%)
  starting transfers between devices  83.3 us (34%)
  local copies, waits for them, and re-layouts  20.2 us (8%)
  matrix products  8.69 us (4%)
  other arithmetic  6.84 us (3%)
    ppermute x30, starting transfers between devices, exchange_in_pairs(): done.append(lax.ppermute(sent, axis, [(i, i ^ step) for i in range(size)]))  41.8 us
    all_to_all x2, waiting for transfers between devices, local(): lax.all_to_all(lax.all_to_all(send_right, 'ch', split_axis=0, concat_axis...  27.5 us
    all_to_all x2, waiting for transfers between devices, local(): lax.all_to_all(lax.all_to_all(send_left, 'ch', split_axis=0, concat_axis=...  26.8 us
    all_to_all x2, waiting for transfers between devices, local(): lax.all_to_all(exchange_in_pairs(returned, 'row', 1, 0), 'ch', split_axis...  24.3 us
    ppermute x30, waiting for transfers between devices, exchange_in_pairs(): done.append(lax.ppermute(sent, axis, [(i, i ^ step) for i in range(size)]))  19.9 us
    all_to_all x2, waiting for transfers between devices, local(): lax.all_to_all(send_left, 'ch', split_axis=0, concat_axis=4, tiled=True)  13.5 us
    all_to_all x2, waiting for transfers between devices, local(): lax.all_to_all(send_right, 'ch', split_axis=0, concat_axis=4, tiled=True)  13.4 us
    all_to_all x2, starting transfers between devices, local(): lax.all_to_all(lax.all_to_all(send_left, 'ch', split_axis=0, concat_axis=...  10 us
  transfers between devices with their start and end apart: 40, of which 18 were waited for; matrix products, arithmetic and copies ran while one was open for 5% of the time, Pallas kernels for 0%

profile of v1, /device:TPU:0, one launch (start us, length us, event | category | flops | bytes accessed | tf_op | source)
XLA Modules:
  0.0 245.2 jit_solution(12804214279707997324)
XLA Ops:
  6.7 2.1 add_bitcast_fusion.1
  10.6 4.3 %all-to-all-start = ((bf16[2,16,4,16,128]{4,3,2,1,0:T(8,128)(2,1)}), bf16[2,16,4,16,128]{4,3,2,1,0:T(8,128)(2,1)S(1)}, u32[]{:S(2)}, u32[]{:S(2)}) async-start(bf16[2,16,4,16,128]{4,3,2,1,0:T(8,128)(2,1)} %bitcast.9), calls=%async_computation | async-start | bytes 1048576 | tf_op jit(solution)/shard_map/all_to_all | solution.py:145
  16.1 7.5 %all-to-all-done = bf16[2,16,4,16,128]{4,3,2,1,0:T(8,128)(2,1)S(1)} async-done(((bf16[2,16,4,16,128]{4,3,2,1,0:T(8,128)(2,1)}), bf16[2,16,4,16,128]{4,3,2,1,0:T(8,128)(2,1)S(1)}, u32[]{:S(2)}, u32[]{:S(2)}) %all-to-all-start) | async-done | bytes 524320 | tf_op jit(solution)/shard_map/all_to_all | solution.py:145
  23.6 3.5 %all-to-all-start.2 = ((bf16[2,16,4,16,128]{4,3,2,1,0:T(8,128)(2,1)}), bf16[2,16,4,16,128]{4,3,2,1,0:T(8,128)(2,1)S(1)}, u32[]{:S(2)}, u32[]{:S(2)}) async-start(bf16[2,16,4,16,128]{4,3,2,1,0:T(8,128)(2,1)} %bitcast.16), calls=%async_computation.2 | async-start | bytes 1048576 | tf_op jit(solution)/shard_map/all_to_all | solution.py:152
  28.0 6.8 %all-to-all-done.2 = bf16[2,16,4,16,128]{4,3,2,1,0:T(8,128)(2,1)S(1)} async-done(((bf16[2,16,4,16,128]{4,3,2,1,0:T(8,128)(2,1)}), bf16[2,16,4,16,128]{4,3,2,1,0:T(8,128)(2,1)S(1)}, u32[]{:S(2)}, u32[]{:S(2)}) %all-to-all-start.2) | async-done | bytes 524320 | tf_op jit(solution)/shard_map/all_to_all | solution.py:152
  34.8 5.8 %all-to-all-start.1 = ((bf16[1,16,4,16,256]{4,3,2,0,1:T(8,128)(2,1)}), bf16[1,16,4,16,256]{4,3,2,0,1:T(8,128)(2,1)S(1)}, u32[]{:S(2)}, u32[]{:S(2)}) async-start(bf16[1,16,4,16,256]{4,3,2,0,1:T(8,128)(2,1)} %bitcast_bitcast_fusion.3), calls=%async_computation.1 | async-start | bytes 1048576 | tf_op jit(solution)/shard_map/all_to_all | solution.py:144
  41.5 13.4 %all-to-all-done.1 = bf16[1,16,4,16,256]{4,3,2,0,1:T(8,128)(2,1)S(1)} async-done(((bf16[1,16,4,16,256]{4,3,2,0,1:T(8,128)(2,1)}), bf16[1,16,4,16,256]{4,3,2,0,1:T(8,128)(2,1)S(1)}, u32[]{:S(2)}, u32[]{:S(2)}) %all-to-all-start.1) | async-done | bytes 524320 | tf_op jit(solution)/shard_map/all_to_all | solution.py:144
  54.9 4.2 %all-to-all-start.3 = ((bf16[1,16,4,16,256]{4,3,2,0,1:T(8,128)(2,1)}), bf16[1,16,4,16,256]{4,3,2,0,1:T(8,128)(2,1)S(1)}, u32[]{:S(2)}, u32[]{:S(2)}) async-start(bf16[1,16,4,16,256]{4,3,2,0,1:T(8,128)(2,1)} %bitcast_bitcast_fusion.2), calls=%async_computation.3 | async-start | bytes 1048576 | tf_op jit(solution)/shard_map/all_to_all | solution.py:151
  59.2 14.1 %all-to-all-done.3 = bf16[1,16,4,16,256]{4,3,2,0,1:T(8,128)(2,1)S(1)} async-done(((bf16[1,16,4,16,256]{4,3,2,0,1:T(8,128)(2,1)}), bf16[1,16,4,16,256]{4,3,2,0,1:T(8,128)(2,1)S(1)}, u32[]{:S(2)}, u32[]{:S(2)}) %all-to-all-start.3) | async-done | bytes 524320 | tf_op jit(solution)/shard_map/all_to_all | solution.py:151
  78.9 2.1 collective-permute-start.5
  81.6 2.5 %collective-permute-start.7 = (f32[4,1,16,2,128]{4,2,3,0,1:T(8,128)S(1)}, f32[4,1,16,2,128]{4,2,3,0,1:T(8,128)S(1)}, u32[]{:S(2)}, u32[]{:S(2)}) collective-permute-start(f32[4,1,16,2,128]{4,2,3,0,1:T(8,128)S(1)} %bitcast.322), channel_id=1, source_target_pairs={{0,16},{2,18},{4,20},{6,22},{8,24},{10,26},{12,28},{14,30},{16,0},... | collective-permute-start | bytes 196616 | tf_op jit(solution)/shard_map/ppermute | solution.py:27
  91.9 4.5 %collective-permute-done.8 = f32[4,1,16,2,128]{4,2,3,0,1:T(8,128)S(1)} collective-permute-done((f32[4,1,16,2,128]{4,2,3,0,1:T(8,128)S(1)}, f32[4,1,16,2,128]{4,2,3,0,1:T(8,128)S(1)}, u32[]{:S(2)}, u32[]{:S(2)}) %collective-permute-start.8) | collective-permute-done | bytes 65568 | tf_op jit(solution)/shard_map/ppermute | solution.py:27
  96.4 2.5 %collective-permute-start.13 = (f32[4,1,16,2,128]{4,2,3,0,1:T(8,128)S(1)}, f32[4,1,16,2,128]{4,2,3,0,1:T(8,128)S(1)}, u32[]{:S(2)}, u32[]{:S(2)}) collective-permute-start(f32[4,1,16,2,128]{4,2,3,0,1:T(8,128)S(1)} %bitcast.310), channel_id=1, source_target_pairs={{0,28},{2,30},{4,24},{6,26},{8,20},{10,22},{12,16},{14,18},{16,12}... | collective-permute-start | bytes 196616 | tf_op jit(solution)/shard_map/ppermute | solution.py:27
  101.1 2.3 collective-permute-done.13
  103.3 2.6 %collective-permute-done.14 = f32[4,1,16,2,128]{4,2,3,0,1:T(8,128)S(1)} collective-permute-done((f32[4,1,16,2,128]{4,2,3,0,1:T(8,128)S(1)}, f32[4,1,16,2,128]{4,2,3,0,1:T(8,128)S(1)}, u32[]{:S(2)}, u32[]{:S(2)}) %collective-permute-start.14) | collective-permute-done | bytes 65568 | tf_op jit(solution)/shard_map/ppermute | solution.py:27
  107.6 3.6 %all-to-all-start.4 = ((f32[64,1,16,2,128]{4,2,0,1,3:T(8,128)}), f32[64,1,16,2,128]{4,2,0,1,3:T(8,128)S(1)}, u32[]{:S(2)}, u32[]{:S(2)}) async-start(f32[64,1,16,2,128]{4,2,0,1,3:T(8,128)} %copy.106), calls=%async_computation.4 | async-start | bytes 2097152 | tf_op jit(solution)/shard_map/all_to_all | solution.py:170
  113.8 11.6 %all-to-all-done.4 = f32[64,1,16,2,128]{4,2,0,1,3:T(8,128)S(1)} async-done(((f32[64,1,16,2,128]{4,2,0,1,3:T(8,128)}), f32[64,1,16,2,128]{4,2,0,1,3:T(8,128)S(1)}, u32[]{:S(2)}, u32[]{:S(2)}) %all-to-all-start.4) | async-done | bytes 1048608 | tf_op jit(solution)/shard_map/all_to_all | solution.py:170
  129.9 3.5 %all-to-all-start.7 = ((bf16[2,16,4,16,128]{4,3,2,1,0:T(8,128)(2,1)}), bf16[2,16,4,16,128]{4,3,2,1,0:T(8,128)(2,1)S(1)}, u32[]{:S(2)}, u32[]{:S(2)}) async-start(bf16[2,16,4,16,128]{4,3,2,1,0:T(8,128)(2,1)} %bitcast.80), calls=%async_computation.7 | async-start | bytes 1048576 | tf_op jit(solution)/shard_map/all_to_all | solution.py:152
  134.6 6.6 %all-to-all-done.7 = bf16[2,16,4,16,128]{4,3,2,1,0:T(8,128)(2,1)S(1)} async-done(((bf16[2,16,4,16,128]{4,3,2,1,0:T(8,128)(2,1)}), bf16[2,16,4,16,128]{4,3,2,1,0:T(8,128)(2,1)S(1)}, u32[]{:S(2)}, u32[]{:S(2)}) %all-to-all-start.7) | async-done | bytes 524320 | tf_op jit(solution)/shard_map/all_to_all | solution.py:152
  141.1 3.5 %all-to-all-start.5 = ((bf16[2,16,4,16,128]{4,3,2,1,0:T(8,128)(2,1)}), bf16[2,16,4,16,128]{4,3,2,1,0:T(8,128)(2,1)S(1)}, u32[]{:S(2)}, u32[]{:S(2)}) async-start(bf16[2,16,4,16,128]{4,3,2,1,0:T(8,128)(2,1)} %bitcast.73), calls=%async_computation.5 | async-start | bytes 1048576 | tf_op jit(solution)/shard_map/all_to_all | solution.py:145
  145.5 6.0 %all-to-all-done.5 = bf16[2,16,4,16,128]{4,3,2,1,0:T(8,128)(2,1)S(1)} async-done(((bf16[2,16,4,16,128]{4,3,2,1,0:T(8,128)(2,1)}), bf16[2,16,4,16,128]{4,3,2,1,0:T(8,128)(2,1)S(1)}, u32[]{:S(2)}, u32[]{:S(2)}) %all-to-all-start.5) | async-done | bytes 524320 | tf_op jit(solution)/shard_map/all_to_all | solution.py:145
  151.5 5.4 %all-to-all-start.8 = ((bf16[1,16,4,16,256]{4,3,2,0,1:T(8,128)(2,1)}), bf16[1,16,4,16,256]{4,3,2,0,1:T(8,128)(2,1)S(1)}, u32[]{:S(2)}, u32[]{:S(2)}) async-start(bf16[1,16,4,16,256]{4,3,2,0,1:T(8,128)(2,1)} %bitcast_bitcast_fusion), calls=%async_computation.8 | async-start | bytes 1048576 | tf_op jit(solution)/shard_map/all_to_all | solution.py:151
  157.8 13.4 %all-to-all-done.8 = bf16[1,16,4,16,256]{4,3,2,0,1:T(8,128)(2,1)S(1)} async-done(((bf16[1,16,4,16,256]{4,3,2,0,1:T(8,128)(2,1)}), bf16[1,16,4,16,256]{4,3,2,0,1:T(8,128)(2,1)S(1)}, u32[]{:S(2)}, u32[]{:S(2)}) %all-to-all-start.8) | async-done | bytes 524320 | tf_op jit(solution)/shard_map/all_to_all | solution.py:151
  171.2 4.2 %all-to-all-start.6 = ((bf16[1,16,4,16,256]{4,3,2,0,1:T(8,128)(2,1)}), bf16[1,16,4,16,256]{4,3,2,0,1:T(8,128)(2,1)S(1)}, u32[]{:S(2)}, u32[]{:S(2)}) async-start(bf16[1,16,4,16,256]{4,3,2,0,1:T(8,128)(2,1)} %bitcast_bitcast_fusion.1), calls=%async_computation.6 | async-start | bytes 1048576 | tf_op jit(solution)/shard_map/all_to_all | solution.py:144
  176.2 13.4 %all-to-all-done.6 = bf16[1,16,4,16,256]{4,3,2,0,1:T(8,128)(2,1)S(1)} async-done(((bf16[1,16,4,16,256]{4,3,2,0,1:T(8,128)(2,1)}), bf16[1,16,4,16,256]{4,3,2,0,1:T(8,128)(2,1)S(1)}, u32[]{:S(2)}, u32[]{:S(2)}) %all-to-all-start.6) | async-done | bytes 524320 | tf_op jit(solution)/shard_map/all_to_all | solution.py:144
  198.9 2.5 %collective-permute-start.22 = (f32[4,1,16,2,128]{4,2,3,0,1:T(8,128)S(1)}, f32[4,1,16,2,128]{4,2,3,0,1:T(8,128)S(1)}, u32[]{:S(2)}, u32[]{:S(2)}) collective-permute-start(f32[4,1,16,2,128]{4,2,3,0,1:T(8,128)S(1)} %bitcast.323), channel_id=1, source_target_pairs={{0,16},{2,18},{4,20},{6,22},{8,24},{10,26},{12,28},{14,30},{16,0},... | collective-permute-start | bytes 196616 | tf_op jit(solution)/shard_map/ppermute | solution.py:27
  209.2 5.2 %collective-permute-done.23 = f32[4,1,16,2,128]{4,2,3,0,1:T(8,128)S(1)} collective-permute-done((f32[4,1,16,2,128]{4,2,3,0,1:T(8,128)S(1)}, f32[4,1,16,2,128]{4,2,3,0,1:T(8,128)S(1)}, u32[]{:S(2)}, u32[]{:S(2)}) %collective-permute-start.23) | collective-permute-done | bytes 65568 | tf_op jit(solution)/shard_map/ppermute | solution.py:27
  216.5 2.2 collective-permute-start.29
  218.8 2.6 %collective-permute-done.28 = f32[4,1,16,2,128]{4,2,3,0,1:T(8,128)S(1)} collective-permute-done((f32[4,1,16,2,128]{4,2,3,0,1:T(8,128)S(1)}, f32[4,1,16,2,128]{4,2,3,0,1:T(8,128)S(1)}, u32[]{:S(2)}, u32[]{:S(2)}) %collective-permute-start.28) | collective-permute-done | bytes 65568 | tf_op jit(solution)/shard_map/ppermute | solution.py:27
  221.4 2.1 collective-permute-done.29
  225.2 3.6 %all-to-all-start.9 = ((f32[64,1,16,2,128]{4,2,1,0,3:T(8,128)}), f32[64,1,16,2,128]{4,2,1,0,3:T(8,128)S(1)}, u32[]{:S(2)}, u32[]{:S(2)}) async-start(f32[64,1,16,2,128]{4,2,1,0,3:T(8,128)} %copy.138), calls=%async_computation.9 | async-start | bytes 2097152 | tf_op jit(solution)/shard_map/all_to_all | solution.py:170
  230.3 12.6 %all-to-all-done.9 = f32[64,1,16,2,128]{4,2,1,0,3:T(8,128)S(1)} async-done(((f32[64,1,16,2,128]{4,2,1,0,3:T(8,128)}), f32[64,1,16,2,128]{4,2,1,0,3:T(8,128)S(1)}, u32[]{:S(2)}, u32[]{:S(2)}) %all-to-all-start.9) | async-done | bytes 1048608 | tf_op jit(solution)/shard_map/all_to_all | solution.py:170
  (190 shorter events, 64.3 us)
Async XLA Ops:
  10.6 13.0 %all-to-all-start = ((bf16[2,16,4,16,128]{4,3,2,1,0:T(8,128)(2,1)}), bf16[2,16,4,16,128]{4,3,2,1,0:T(8,128)(2,1)S(1)}, u32[]{:S(2)}, u32[]{:S(2)}) async-start(bf16[2,16,4,16,128]{4,3,2,1,0:T(8,128)(2,1)} %bitcast.9), calls=%async_computation | async-start | bytes 1048576 | tf_op jit(solution)/shard_map/all_to_all | solution.py:145
  23.6 11.2 %all-to-all-start.2 = ((bf16[2,16,4,16,128]{4,3,2,1,0:T(8,128)(2,1)}), bf16[2,16,4,16,128]{4,3,2,1,0:T(8,128)(2,1)S(1)}, u32[]{:S(2)}, u32[]{:S(2)}) async-start(bf16[2,16,4,16,128]{4,3,2,1,0:T(8,128)(2,1)} %bitcast.16), calls=%async_computation.2 | async-start | bytes 1048576 | tf_op jit(solution)/shard_map/all_to_all | solution.py:152
  34.8 20.1 %all-to-all-start.1 = ((bf16[1,16,4,16,256]{4,3,2,0,1:T(8,128)(2,1)}), bf16[1,16,4,16,256]{4,3,2,0,1:T(8,128)(2,1)S(1)}, u32[]{:S(2)}, u32[]{:S(2)}) async-start(bf16[1,16,4,16,256]{4,3,2,0,1:T(8,128)(2,1)} %bitcast_bitcast_fusion.3), calls=%async_computation.1 | async-start | bytes 1048576 | tf_op jit(solution)/shard_map/all_to_all | solution.py:144
  54.9 18.4 %all-to-all-start.3 = ((bf16[1,16,4,16,256]{4,3,2,0,1:T(8,128)(2,1)}), bf16[1,16,4,16,256]{4,3,2,0,1:T(8,128)(2,1)S(1)}, u32[]{:S(2)}, u32[]{:S(2)}) async-start(bf16[1,16,4,16,256]{4,3,2,0,1:T(8,128)(2,1)} %bitcast_bitcast_fusion.2), calls=%async_computation.3 | async-start | bytes 1048576 | tf_op jit(solution)/shard_map/all_to_all | solution.py:151
  76.9 7.2 %collective-permute-start.3 = (f32[4,1,16,2,128]{4,2,3,0,1:T(8,128)S(1)}, f32[4,1,16,2,128]{4,2,3,0,1:T(8,128)S(1)}, u32[]{:S(2)}, u32[]{:S(2)}) collective-permute-start(f32[4,1,16,2,128]{4,2,3,0,1:T(8,128)S(1)} %bitcast.330), channel_id=1, source_target_pairs={{0,8},{2,10},{4,12},{6,14},{8,0},{10,2},{12,4},{14,6},{16,24},{18,... | collective-permute-start | bytes 196616 | tf_op jit(solution)/shard_map/ppermute | solution.py:27
  78.9 7.5 %collective-permute-start.5 = (f32[4,1,16,2,128]{4,2,3,0,1:T(8,128)S(1)}, f32[4,1,16,2,128]{4,2,3,0,1:T(8,128)S(1)}, u32[]{:S(2)}, u32[]{:S(2)}) collective-permute-start(f32[4,1,16,2,128]{4,2,3,0,1:T(8,128)S(1)} %bitcast.326), channel_id=1, source_target_pairs={{0,12},{2,14},{4,8},{6,10},{8,4},{10,6},{12,0},{14,2},{16,28},{18,... | collective-permute-start | bytes 196616 | tf_op jit(solution)/shard_map/ppermute | solution.py:27
  81.0 7.1 %collective-permute-start.6 = (f32[4,1,16,2,128]{4,2,3,0,1:T(8,128)S(1)}, f32[4,1,16,2,128]{4,2,3,0,1:T(8,128)S(1)}, u32[]{:S(2)}, u32[]{:S(2)}) collective-permute-start(f32[4,1,16,2,128]{4,2,3,0,1:T(8,128)S(1)} %bitcast.324), channel_id=1, source_target_pairs={{0,14},{2,12},{4,10},{6,8},{8,6},{10,4},{12,2},{14,0},{16,30},{18,... | collective-permute-start | bytes 196616 | tf_op jit(solution)/shard_map/ppermute | solution.py:27
  81.6 8.5 %collective-permute-start.7 = (f32[4,1,16,2,128]{4,2,3,0,1:T(8,128)S(1)}, f32[4,1,16,2,128]{4,2,3,0,1:T(8,128)S(1)}, u32[]{:S(2)}, u32[]{:S(2)}) collective-permute-start(f32[4,1,16,2,128]{4,2,3,0,1:T(8,128)S(1)} %bitcast.322), channel_id=1, source_target_pairs={{0,16},{2,18},{4,20},{6,22},{8,24},{10,26},{12,28},{14,30},{16,0},... | collective-permute-start | bytes 196616 | tf_op jit(solution)/shard_map/ppermute | solution.py:27
  84.1 12.3 %collective-permute-start.8 = (f32[4,1,16,2,128]{4,2,3,0,1:T(8,128)S(1)}, f32[4,1,16,2,128]{4,2,3,0,1:T(8,128)S(1)}, u32[]{:S(2)}, u32[]{:S(2)}) collective-permute-start(f32[4,1,16,2,128]{4,2,3,0,1:T(8,128)S(1)} %bitcast.320), channel_id=1, source_target_pairs={{0,18},{2,16},{4,22},{6,20},{8,26},{10,24},{12,30},{14,28},{16,2},... | collective-permute-start | bytes 196616 | tf_op jit(solution)/shard_map/ppermute | solution.py:27
  84.5 14.6 %collective-permute-start.9 = (f32[4,1,16,2,128]{4,2,3,0,1:T(8,128)S(1)}, f32[4,1,16,2,128]{4,2,3,0,1:T(8,128)S(1)}, u32[]{:S(2)}, u32[]{:S(2)}) collective-permute-start(f32[4,1,16,2,128]{4,2,3,0,1:T(8,128)S(1)} %bitcast.318), channel_id=1, source_target_pairs={{0,20},{2,22},{4,16},{6,18},{8,28},{10,30},{12,24},{14,26},{16,4},... | collective-permute-start | bytes 196616 | tf_op jit(solution)/shard_map/ppermute | solution.py:27
  86.4 14.6 %collective-permute-start.10 = (f32[4,1,16,2,128]{4,2,3,0,1:T(8,128)S(1)}, f32[4,1,16,2,128]{4,2,3,0,1:T(8,128)S(1)}, u32[]{:S(2)}, u32[]{:S(2)}) collective-permute-start(f32[4,1,16,2,128]{4,2,3,0,1:T(8,128)S(1)} %bitcast.316), channel_id=1, source_target_pairs={{0,22},{2,20},{4,18},{6,16},{8,30},{10,28},{12,26},{14,24},{16,6},... | collective-permute-start | bytes 196616 | tf_op jit(solution)/shard_map/ppermute | solution.py:27
  88.1 12.9 %collective-permute-start.11 = (f32[4,1,16,2,128]{4,2,3,0,1:T(8,128)S(1)}, f32[4,1,16,2,128]{4,2,3,0,1:T(8,128)S(1)}, u32[]{:S(2)}, u32[]{:S(2)}) collective-permute-start(f32[4,1,16,2,128]{4,2,3,0,1:T(8,128)S(1)} %bitcast.314), channel_id=1, source_target_pairs={{0,24},{2,26},{4,28},{6,30},{8,16},{10,18},{12,20},{14,22},{16,8},... | collective-permute-start | bytes 196616 | tf_op jit(solution)/shard_map/ppermute | solution.py:27
  90.1 10.9 %collective-permute-start.12 = (f32[4,1,16,2,128]{4,2,3,0,1:T(8,128)S(1)}, f32[4,1,16,2,128]{4,2,3,0,1:T(8,128)S(1)}, u32[]{:S(2)}, u32[]{:S(2)}) collective-permute-start(f32[4,1,16,2,128]{4,2,3,0,1:T(8,128)S(1)} %bitcast.312), channel_id=1, source_target_pairs={{0,26},{2,24},{4,30},{6,28},{8,18},{10,16},{12,22},{14,20},{16,10}... | collective-permute-start | bytes 196616 | tf_op jit(solution)/shard_map/ppermute | solution.py:27
  96.4 7.0 %collective-permute-start.13 = (f32[4,1,16,2,128]{4,2,3,0,1:T(8,128)S(1)}, f32[4,1,16,2,128]{4,2,3,0,1:T(8,128)S(1)}, u32[]{:S(2)}, u32[]{:S(2)}) collective-permute-start(f32[4,1,16,2,128]{4,2,3,0,1:T(8,128)S(1)} %bitcast.310), channel_id=1, source_target_pairs={{0,28},{2,30},{4,24},{6,26},{8,20},{10,22},{12,16},{14,18},{16,12}... | collective-permute-start | bytes 196616 | tf_op jit(solution)/shard_map/ppermute | solution.py:27
  99.1 6.8 %collective-permute-start.14 = (f32[4,1,16,2,128]{4,2,3,0,1:T(8,128)S(1)}, f32[4,1,16,2,128]{4,2,3,0,1:T(8,128)S(1)}, u32[]{:S(2)}, u32[]{:S(2)}) collective-permute-start(f32[4,1,16,2,128]{4,2,3,0,1:T(8,128)S(1)} %bitcast.308), channel_id=1, source_target_pairs={{0,30},{2,28},{4,26},{6,24},{8,22},{10,20},{12,18},{14,16},{16,14}... | collective-permute-start | bytes 196616 | tf_op jit(solution)/shard_map/ppermute | solution.py:27
  107.6 17.8 %all-to-all-start.4 = ((f32[64,1,16,2,128]{4,2,0,1,3:T(8,128)}), f32[64,1,16,2,128]{4,2,0,1,3:T(8,128)S(1)}, u32[]{:S(2)}, u32[]{:S(2)}) async-start(f32[64,1,16,2,128]{4,2,0,1,3:T(8,128)} %copy.106), calls=%async_computation.4 | async-start | bytes 2097152 | tf_op jit(solution)/shard_map/all_to_all | solution.py:170
  129.9 11.3 %all-to-all-start.7 = ((bf16[2,16,4,16,128]{4,3,2,1,0:T(8,128)(2,1)}), bf16[2,16,4,16,128]{4,3,2,1,0:T(8,128)(2,1)S(1)}, u32[]{:S(2)}, u32[]{:S(2)}) async-start(bf16[2,16,4,16,128]{4,3,2,1,0:T(8,128)(2,1)} %bitcast.80), calls=%async_computation.7 | async-start | bytes 1048576 | tf_op jit(solution)/shard_map/all_to_all | solution.py:152
  141.1 10.4 %all-to-all-start.5 = ((bf16[2,16,4,16,128]{4,3,2,1,0:T(8,128)(2,1)}), bf16[2,16,4,16,128]{4,3,2,1,0:T(8,128)(2,1)S(1)}, u32[]{:S(2)}, u32[]{:S(2)}) async-start(bf16[2,16,4,16,128]{4,3,2,1,0:T(8,128)(2,1)} %bitcast.73), calls=%async_computation.5 | async-start | bytes 1048576 | tf_op jit(solution)/shard_map/all_to_all | solution.py:145
  151.5 19.7 %all-to-all-start.8 = ((bf16[1,16,4,16,256]{4,3,2,0,1:T(8,128)(2,1)}), bf16[1,16,4,16,256]{4,3,2,0,1:T(8,128)(2,1)S(1)}, u32[]{:S(2)}, u32[]{:S(2)}) async-start(bf16[1,16,4,16,256]{4,3,2,0,1:T(8,128)(2,1)} %bitcast_bitcast_fusion), calls=%async_computation.8 | async-start | bytes 1048576 | tf_op jit(solution)/shard_map/all_to_all | solution.py:151
  171.2 18.4 %all-to-all-start.6 = ((bf16[1,16,4,16,256]{4,3,2,0,1:T(8,128)(2,1)}), bf16[1,16,4,16,256]{4,3,2,0,1:T(8,128)(2,1)S(1)}, u32[]{:S(2)}, u32[]{:S(2)}) async-start(bf16[1,16,4,16,256]{4,3,2,0,1:T(8,128)(2,1)} %bitcast_bitcast_fusion.1), calls=%async_computation.6 | async-start | bytes 1048576 | tf_op jit(solution)/shard_map/all_to_all | solution.py:144
  194.2 7.2 %collective-permute-start.18 = (f32[4,1,16,2,128]{4,2,3,0,1:T(8,128)S(1)}, f32[4,1,16,2,128]{4,2,3,0,1:T(8,128)S(1)}, u32[]{:S(2)}, u32[]{:S(2)}) collective-permute-start(f32[4,1,16,2,128]{4,2,3,0,1:T(8,128)S(1)} %bitcast.331), channel_id=1, source_target_pairs={{0,8},{2,10},{4,12},{6,14},{8,0},{10,2},{12,4},{14,6},{16,24},{18,... | collective-permute-start | bytes 196616 | tf_op jit(solution)/shard_map/ppermute | solution.py:27
  196.2 7.5 %collective-permute-start.20 = (f32[4,1,16,2,128]{4,2,3,0,1:T(8,128)S(1)}, f32[4,1,16,2,128]{4,2,3,0,1:T(8,128)S(1)}, u32[]{:S(2)}, u32[]{:S(2)}) collective-permute-start(f32[4,1,16,2,128]{4,2,3,0,1:T(8,128)S(1)} %bitcast.327), channel_id=1, source_target_pairs={{0,12},{2,14},{4,8},{6,10},{8,4},{10,6},{12,0},{14,2},{16,28},{18,... | collective-permute-start | bytes 196616 | tf_op jit(solution)/shard_map/ppermute | solution.py:27
  198.3 7.1 %collective-permute-start.21 = (f32[4,1,16,2,128]{4,2,3,0,1:T(8,128)S(1)}, f32[4,1,16,2,128]{4,2,3,0,1:T(8,128)S(1)}, u32[]{:S(2)}, u32[]{:S(2)}) collective-permute-start(f32[4,1,16,2,128]{4,2,3,0,1:T(8,128)S(1)} %bitcast.325), channel_id=1, source_target_pairs={{0,14},{2,12},{4,10},{6,8},{8,6},{10,4},{12,2},{14,0},{16,30},{18,... | collective-permute-start | bytes 196616 | tf_op jit(solution)/shard_map/ppermute | solution.py:27
  198.9 8.5 %collective-permute-start.22 = (f32[4,1,16,2,128]{4,2,3,0,1:T(8,128)S(1)}, f32[4,1,16,2,128]{4,2,3,0,1:T(8,128)S(1)}, u32[]{:S(2)}, u32[]{:S(2)}) collective-permute-start(f32[4,1,16,2,128]{4,2,3,0,1:T(8,128)S(1)} %bitcast.323), channel_id=1, source_target_pairs={{0,16},{2,18},{4,20},{6,22},{8,24},{10,26},{12,28},{14,30},{16,0},... | collective-permute-start | bytes 196616 | tf_op jit(solution)/shard_map/ppermute | solution.py:27
  201.4 13.0 %collective-permute-start.23 = (f32[4,1,16,2,128]{4,2,3,0,1:T(8,128)S(1)}, f32[4,1,16,2,128]{4,2,3,0,1:T(8,128)S(1)}, u32[]{:S(2)}, u32[]{:S(2)}) collective-permute-start(f32[4,1,16,2,128]{4,2,3,0,1:T(8,128)S(1)} %bitcast.321), channel_id=1, source_target_pairs={{0,18},{2,16},{4,22},{6,20},{8,26},{10,24},{12,30},{14,28},{16,2},... | collective-permute-start | bytes 196616 | tf_op jit(solution)/shard_map/ppermute | solution.py:27
  201.8 14.6 %collective-permute-start.24 = (f32[4,1,16,2,128]{4,2,3,0,1:T(8,128)S(1)}, f32[4,1,16,2,128]{4,2,3,0,1:T(8,128)S(1)}, u32[]{:S(2)}, u32[]{:S(2)}) collective-permute-start(f32[4,1,16,2,128]{4,2,3,0,1:T(8,128)S(1)} %bitcast.319), channel_id=1, source_target_pairs={{0,20},{2,22},{4,16},{6,18},{8,28},{10,30},{12,24},{14,26},{16,4},... | collective-permute-start | bytes 196616 | tf_op jit(solution)/shard_map/ppermute | solution.py:27
  203.8 14.9 %collective-permute-start.25 = (f32[4,1,16,2,128]{4,2,3,0,1:T(8,128)S(1)}, f32[4,1,16,2,128]{4,2,3,0,1:T(8,128)S(1)}, u32[]{:S(2)}, u32[]{:S(2)}) collective-permute-start(f32[4,1,16,2,128]{4,2,3,0,1:T(8,128)S(1)} %bitcast.317), channel_id=1, source_target_pairs={{0,22},{2,20},{4,18},{6,16},{8,30},{10,28},{12,26},{14,24},{16,6},... | collective-permute-start | bytes 196616 | tf_op jit(solution)/shard_map/ppermute | solution.py:27
  205.4 13.3 %collective-permute-start.26 = (f32[4,1,16,2,128]{4,2,3,0,1:T(8,128)S(1)}, f32[4,1,16,2,128]{4,2,3,0,1:T(8,128)S(1)}, u32[]{:S(2)}, u32[]{:S(2)}) collective-permute-start(f32[4,1,16,2,128]{4,2,3,0,1:T(8,128)S(1)} %bitcast.315), channel_id=1, source_target_pairs={{0,24},{2,26},{4,28},{6,30},{8,16},{10,18},{12,20},{14,22},{16,8},... | collective-permute-start | bytes 196616 | tf_op jit(solution)/shard_map/ppermute | solution.py:27
  207.5 11.3 %collective-permute-start.27 = (f32[4,1,16,2,128]{4,2,3,0,1:T(8,128)S(1)}, f32[4,1,16,2,128]{4,2,3,0,1:T(8,128)S(1)}, u32[]{:S(2)}, u32[]{:S(2)}) collective-permute-start(f32[4,1,16,2,128]{4,2,3,0,1:T(8,128)S(1)} %bitcast.313), channel_id=1, source_target_pairs={{0,26},{2,24},{4,30},{6,28},{8,18},{10,16},{12,22},{14,20},{16,10}... | collective-permute-start | bytes 196616 | tf_op jit(solution)/shard_map/ppermute | solution.py:27
  214.4 7.0 %collective-permute-start.28 = (f32[4,1,16,2,128]{4,2,3,0,1:T(8,128)S(1)}, f32[4,1,16,2,128]{4,2,3,0,1:T(8,128)S(1)}, u32[]{:S(2)}, u32[]{:S(2)}) collective-permute-start(f32[4,1,16,2,128]{4,2,3,0,1:T(8,128)S(1)} %bitcast.311), channel_id=1, source_target_pairs={{0,28},{2,30},{4,24},{6,26},{8,20},{10,22},{12,16},{14,18},{16,12}... | collective-permute-start | bytes 196616 | tf_op jit(solution)/shard_map/ppermute | solution.py:27
  216.5 7.1 %collective-permute-start.29 = (f32[4,1,16,2,128]{4,2,3,0,1:T(8,128)S(1)}, f32[4,1,16,2,128]{4,2,3,0,1:T(8,128)S(1)}, u32[]{:S(2)}, u32[]{:S(2)}) collective-permute-start(f32[4,1,16,2,128]{4,2,3,0,1:T(8,128)S(1)} %bitcast.309), channel_id=1, source_target_pairs={{0,30},{2,28},{4,26},{6,24},{8,22},{10,20},{12,18},{14,16},{16,14}... | collective-permute-start | bytes 196616 | tf_op jit(solution)/shard_map/ppermute | solution.py:27
  225.2 17.7 %all-to-all-start.9 = ((f32[64,1,16,2,128]{4,2,1,0,3:T(8,128)}), f32[64,1,16,2,128]{4,2,1,0,3:T(8,128)S(1)}, u32[]{:S(2)}, u32[]{:S(2)}) async-start(f32[64,1,16,2,128]{4,2,1,0,3:T(8,128)} %copy.138), calls=%async_computation.9 | async-start | bytes 2097152 | tf_op jit(solution)/shard_map/all_to_all | solution.py:170
  (16 other events, 180.4 us)
